TPU v7x, 64 devices: a 2x2x8 block of a 4x4x8 slice. The times are simulated.
64 devices in a mesh: rep: 8 (over x, y, core), dp: 8 (over z).
Axes of the slice: x: 2, y: 2, z: 8, core: 2. Of those that a mesh axis runs over, the one named last changes fastest.
The devices are a block of a 4x4x8 slice.
Arguments:
- g_w_gate: bfloat16 [64, 2, 640, 1536], P(('rep', 'dp')), parts along dimension 0
- g_w_up: bfloat16 [64, 2, 640, 1536], P(('rep', 'dp')), parts along dimension 0
- g_w_down: bfloat16 [64, 2, 1536, 640], P(('rep', 'dp')), parts along dimension 0
- w_gate: bfloat16 [2, 640, 1536], replicated
- w_up: bfloat16 [2, 640, 1536], replicated
- w_down: bfloat16 [2, 1536, 640], replicated
- m_w_gate: float32 [2, 640, 1536], P(None, 'dp')
- m_w_up: float32 [2, 640, 1536], P(None, 'dp')
- m_w_down: float32 [2, 1536, 640], P(None, 'dp')
- v_w_gate: float32 [2, 640, 1536], P(None, 'dp')
- v_w_up: float32 [2, 640, 1536], P(None, 'dp')
- v_w_down: float32 [2, 1536, 640], P(None, 'dp')
Outputs:
- output 1: bfloat16 [16, 640, 1536], P('rep'), parts along dimension 0
- output 2: bfloat16 [16, 640, 1536], P('rep'), parts along dimension 0
- output 3: bfloat16 [16, 1536, 640], P('rep'), parts along dimension 0
- output 4: float32 [16, 640, 1536], P('rep', 'dp'), parts along dimension 0
- output 5: float32 [16, 640, 1536], P('rep', 'dp'), parts along dimension 0
- output 6: float32 [16, 1536, 640], P('rep', 'dp'), parts along dimension 0
- output 7: float32 [16, 640, 1536], P('rep', 'dp'), parts along dimension 0
- output 8: float32 [16, 640, 1536], P('rep', 'dp'), parts along dimension 0
- output 9: float32 [16, 1536, 640], P('rep', 'dp'), parts along dimension 0
There are 8 independent parts. A program takes and returns all parts, laid end to end along the dimension named above; an argument that names none is the same for every part.
All inputs are finite; a program needn't handle non-finite values.
Results may differ from a plain program's by a relative error of at most 0.022.
Values are sent between devices in bfloat16 or wider.
A program may use at most 768 MiB of HBM per device.

v0:
```python
import jax
import jax.numpy as jnp
from jax import lax
from jax.sharding import PartitionSpec as P


def adamw(w, m, v, g):
    m = 0.9 * m + 0.1 * g
    v = 0.95 * v + 0.05 * g * g
    step = m * lax.rsqrt(v + 1e-8) + 0.1 * w
    return (w - 0.02 * step).astype(jnp.bfloat16), m, v


def clipped(gradients, sum_of_squares, count):
    factor = jnp.minimum(1.0, 0.5 * lax.rsqrt(sum_of_squares / count + 1e-30))
    return [g * factor for g in gradients]


def solution(mesh):
    def step(*arrays):
        terms, weights, m, v = (arrays[i : i + 3] for i in (0, 3, 6, 9))
        gradients = [lax.psum_scatter(t[0], "dp", scatter_dimension=1, tiled=True).astype(jnp.float32) for t in terms]
        squares = lax.psum(sum(jnp.sum(g * g) for g in gradients), "dp")
        gradients = clipped(gradients, squares, lax.psum(1, "dp") * sum(g.size for g in gradients))
        me = lax.axis_index("dp")
        own = [lax.dynamic_slice_in_dim(w, me * one.shape[1], one.shape[1], 1).astype(jnp.float32) for w, one in zip(weights, m, strict=True)]
        new = [adamw(w, m, v, g) for w, m, v, g in zip(own, m, v, gradients, strict=True)]
        whole = [lax.all_gather(one[0], "dp", axis=1, tiled=True) for one in new]
        return (*whole, *(one[1] for one in new), *(one[2] for one in new))

    all_of, cut = P(None, None, None), P(None, "dp", None)
    return jax.shard_map(
        step,
        mesh=mesh,
        in_specs=(P(("rep", "dp"), None, None, None),) * 3 + (all_of,) * 3 + (cut,) * 6,
        out_specs=(P("rep", None, None),) * 3 + (P("rep", "dp", None),) * 6,
        check_vma=False,
    )
```

profile of v0, /device:TPU:22, one launch (start us, length us, event | category | flops | bytes accessed | tf_op | source)
XLA Modules:
  0.0 352.7 jit_solution(2342820115403836548)
XLA Ops:
  7.2 0.1 reduce-scatter.4.cloned.1.call-start
  7.3 0.7 reduce-scatter.4.cloned.1.call-update
  8.0 0.1 reduce-scatter.6.cloned.1.call-start
  8.1 0.0 copy-start.4
  8.1 0.0 copy-start.5
  8.1 0.7 reduce-scatter.6.cloned.1.call-update
  8.8 0.1 reduce-scatter.8.cloned.1.call-start
  8.9 0.7 reduce-scatter.8.cloned.1.call-update
  9.6 0.0 copy-start.6
  9.6 0.1 all-gather.8.cloned.1.call-start
  9.7 54.0 %reduce-scatter.4.cloned.1.call-done = bf16[2,80,1536]{2,1,0:T(8,128)(2,1)} async-done(((bf16[2,640,1536]{2,1,0:T(8,128)(2,1)}), bf16[2,80,1536]{2,1,0:T(8,128)(2,1)}) %reduce-scatter.4.cloned.1.call-update) | async-done | bytes 491536 | tf_op jit(solution)/shard_map/reduce_scatter | solution.py:22
  63.7 0.0 copy-start.3
  63.7 2.0 fusion.9
  65.7 49.0 %reduce-scatter.6.cloned.1.call-done = bf16[2,80,1536]{2,1,0:T(8,128)(2,1)} async-done(((bf16[2,640,1536]{2,1,0:T(8,128)(2,1)}), bf16[2,80,1536]{2,1,0:T(8,128)(2,1)}) %reduce-scatter.6.cloned.1.call-update) | async-done | bytes 491536 | tf_op jit(solution)/shard_map/reduce_scatter | solution.py:22
  114.6 1.9 fusion.10
  117.8 47.8 %reduce-scatter.8.cloned.1.call-done = bf16[2,192,640]{2,1,0:T(8,128)(2,1)} async-done(((bf16[2,1536,640]{2,1,0:T(8,128)(2,1)}), bf16[2,192,640]{2,1,0:T(8,128)(2,1)}) %reduce-scatter.8.cloned.1.call-update) | async-done | bytes 491536 | tf_op jit(solution)/shard_map/reduce_scatter | solution.py:22
  165.6 1.9 fusion.11
  168.2 16.1 %psum.7 = f32[]{:T(128)} all-reduce(f32[]{:T(128)S(6)} %add.65), channel_id=1, replica_groups=mesh['rep'=8,'dp'=8] {'dp'}, use_global_device_ids=true, to_apply=%region_6.0 | all-reduce | flops 1 | bytes 8 | tf_op jit(solution)/shard_map/psum | solution.py:23
  185.0 0.0 copy-done.4
  185.0 0.0 copy-done.5
  185.0 2.9 fusion.17
  187.9 0.0 copy-start.2
  187.9 0.0 copy-start.7
  187.9 0.1 all-gather.8.cloned.1.call-update
  187.9 0.1 all-gather.4.cloned.1.call-start
  188.0 0.0 copy-done.6
  188.0 0.0 copy-done.3
  188.0 3.2 fusion.8
  191.2 0.1 all-gather.4.cloned.1.call-update
  191.3 0.1 all-gather.6.cloned.1.call-start
  191.3 0.0 copy-done.2
  191.3 0.0 copy-done.7
  191.4 3.1 fusion.14
  194.4 0.1 all-gather.6.cloned.1.call-update
  194.5 42.3 %all-gather.8.cloned.1.call-done = bf16[2,1536,640]{2,1,0:T(8,128)(2,1)} async-done(((bf16[2,192,640]{2,1,0:T(8,128)(2,1)}), bf16[2,1536,640]{2,1,0:T(8,128)(2,1)}) %all-gather.8.cloned.1.call-update) | async-done | bytes 3932176 | tf_op jit(solution)/shard_map/all_gather | solution.py:28
  236.8 49.5 %all-gather.4.cloned.1.call-done = bf16[2,640,1536]{2,1,0:T(8,128)(2,1)} async-done(((bf16[2,80,1536]{2,1,0:T(8,128)(2,1)}), bf16[2,640,1536]{2,1,0:T(8,128)(2,1)}) %all-gather.4.cloned.1.call-update) | async-done | bytes 3932176 | tf_op jit(solution)/shard_map/all_gather | solution.py:28
  286.4 49.5 %all-gather.6.cloned.1.call-done = bf16[2,640,1536]{2,1,0:T(8,128)(2,1)} async-done(((bf16[2,80,1536]{2,1,0:T(8,128)(2,1)}), bf16[2,640,1536]{2,1,0:T(8,128)(2,1)}) %all-gather.6.cloned.1.call-update) | async-done | bytes 3932176 | tf_op jit(solution)/shard_map/all_gather | solution.py:28
  335.9 0.0 copy-start.1
  335.9 4.5 %copy.24 = bf16[2,640,1536]{2,1,0:T(8,128)(2,1)} copy(bf16[2,640,1536]{2,1,0:T(8,128)(2,1)} %all-gather.4.cloned.1.call-done) | data formatting | bytes 7864320
  340.4 0.0 copy-done.1
  340.4 0.0 copy-start
  340.4 2.0 copy.25
  342.4 1.5 copy-done
  343.9 1.9 copy.26
Async XLA Ops:
  7.2 56.5 %reduce-scatter.4.cloned.1.call-start = ((), (), s32[]{:S(2)}) async-start(), calls=%async_computation.3 | async-start | bytes 4423680 | tf_op jit(solution)/shard_map/reduce_scatter | solution.py:22
  8.0 106.7 %reduce-scatter.6.cloned.1.call-start = ((), (), s32[]{:S(2)}) async-start(), calls=%async_computation.4 | async-start | bytes 4423680 | tf_op jit(solution)/shard_map/reduce_scatter | solution.py:22
  8.1 176.9 %copy-start.4 = (f32[2,192,640]{2,1,0:T(8,128)S(1)}, f32[2,192,640]{2,1,0:T(8,128)}, u32[]{:S(2)}) copy-start(f32[2,192,640]{2,1,0:T(8,128)} %param.23) | copy-start | bytes 2949124
  8.1 176.9 %copy-start.5 = (f32[2,192,640]{2,1,0:T(8,128)S(1)}, f32[2,192,640]{2,1,0:T(8,128)}, u32[]{:S(2)}) copy-start(f32[2,192,640]{2,1,0:T(8,128)} %param.20) | copy-start | bytes 2949124
  8.8 156.8 %reduce-scatter.8.cloned.1.call-start = ((), (), s32[]{:S(2)}) async-start(), calls=%async_computation.5 | async-start | bytes 4423680 | tf_op jit(solution)/shard_map/reduce_scatter | solution.py:22
  9.6 178.4 %copy-start.6 = (f32[2,80,1536]{2,1,0:T(8,128)S(1)}, f32[2,80,1536]{2,1,0:T(8,128)}, u32[]{:S(2)}) copy-start(f32[2,80,1536]{2,1,0:T(8,128)} %param.21) | copy-start | bytes 2949124
  9.6 227.2 %all-gather.8.cloned.1.call-start = ((), (), s32[]{:S(2)}) async-start(), calls=%async_computation.8 | async-start | bytes 4423680 | tf_op jit(solution)/shard_map/all_gather | solution.py:28
  63.7 124.3 %copy-start.3 = (bf16[2,80,1536]{2,1,0:T(8,128)(2,1)S(1)}, bf16[2,80,1536]{2,1,0:T(8,128)(2,1)}, u32[]{:S(2)}) copy-start(bf16[2,80,1536]{2,1,0:T(8,128)(2,1)} %reduce-scatter.4.cloned.1.call-done) | copy-start | bytes 1474564
  187.9 3.5 copy-start.2
  187.9 3.5 copy-start.7
  187.9 98.4 %all-gather.4.cloned.1.call-start = ((), (), s32[]{:S(2)}) async-start(), calls=%async_computation.6 | async-start | bytes 4423680 | tf_op jit(solution)/shard_map/all_gather | solution.py:28
  191.3 144.6 %all-gather.6.cloned.1.call-start = ((), (), s32[]{:S(2)}) async-start(), calls=%async_computation.7 | async-start | bytes 4423680 | tf_op jit(solution)/shard_map/all_gather | solution.py:28
  335.9 4.5 %copy-start.1 = (bf16[2,640,1536]{2,1,0:T(8,128)(2,1)S(1)}, bf16[2,640,1536]{2,1,0:T(8,128)(2,1)}, u32[]{:S(2)}) copy-start(bf16[2,640,1536]{2,1,0:T(8,128)(2,1)} %all-gather.6.cloned.1.call-done) | copy-start | bytes 11796484
  340.4 3.5 %copy-start = (bf16[2,1536,640]{2,1,0:T(8,128)(2,1)S(1)}, bf16[2,1536,640]{2,1,0:T(8,128)(2,1)}, u32[]{:S(2)}) copy-start(bf16[2,1536,640]{2,1,0:T(8,128)(2,1)} %all-gather.8.cloned.1.call-done) | copy-start | bytes 11796484
Sparse Core Ops, SparseCore 0:
  10.4 53.2 reduce-scatter.3
  66.1 48.5 reduce-scatter.5
  117.0 48.5 reduce-scatter.7
  188.1 48.7 all-gather.7
  238.8 47.4 all-gather.3
  288.4 47.4 all-gather.5
where the time goes:
time: 354 us; the launch traced here: 353 us
  waiting for transfers between devices  295 us (83%)
  between operations  16.9 us (5%)
  blocking collectives  16.1 us (5%)
  other arithmetic  14.8 us (4%)
  local copies, waits for them, and re-layouts  9.93 us (3%)
    reduce_scatter x3, waiting for transfers between devices, step(): lax.psum_scatter(t[0], 'dp', scatter_dimension=1, tiled=True)  151 us
    all_gather x3, waiting for transfers between devices, step(): whole = [lax.all_gather(one[0], 'dp', axis=1, tiled=True) for one in new]  141 us
    psum x1, blocking collectives, step(): squares = lax.psum(sum((jnp.sum(g * g) for g in gradients)), 'dp')  16.1 us
    unnamed x19, local copies, waits for them, and re-layouts  9.93 us
    convert_element_type x3, other arithmetic, adamw(): return ((w - 0.02 * step).astype(jnp.bfloat16), m, v)  9.11 us
  transfers between devices with their start and end apart: 6, of which 6 were waited for; matrix products, arithmetic and copies ran while one was open for 3% of the time, Pallas kernels for 0%

commit v1 on v0

v1 whole, which is shorter than its diff:
```python
import functools

import jax
import jax.numpy as jnp
from jax import lax
from jax.experimental import pallas as pl
from jax.experimental.pallas import tpu as pltpu
from jax.sharding import PartitionSpec as P

WAYS = (1, -1)


def row_blocks(rows, columns):
    best = 16
    for step in range(16, rows + 1, 16):
        if rows % step == 0 and step * columns <= 32 * 1024:
            best = step
    return best


def kernel(n, layers, count, *refs):
    kinds = 3
    g, w, m, v = (refs[i : i + kinds] for i in range(0, 4 * kinds, kinds))
    refs = refs[4 * kinds :]
    new_w, new_m, new_v = (refs[i : i + kinds] for i in range(0, 3 * kinds, kinds))
    refs = refs[3 * kinds :]
    own, term, got = (refs[i : i + kinds] for i in range(0, 3 * kinds, kinds))
    squares, rs_send, rs_recv, ag_send, ag_recv, sq_send, sq_recv, load_own, load_term, load_state = refs[3 * kinds :]
    half = n // 2
    me = lax.axis_index("dp")
    rows = [ref.shape[1] for ref in own]
    across = [lax.rem(me + way + n, n) for way in WAYS]
    pairs = [(layer, kind) for layer in range(layers) for kind in range(kinds)]

    def at(way, steps):
        return lax.rem(me + WAYS[way] * steps + n, n)

    def block(chunk, kind):
        return pl.ds(pl.multiple_of(chunk * rows[kind], 16), rows[kind])

    def remote(src, dst, send, recv, to):
        copy = pltpu.make_async_remote_copy(src, dst, send, recv, device_id={"dp": to}, device_id_type=pl.DeviceIdType.MESH)
        return copy

    barrier = pltpu.get_barrier_semaphore()
    for to in across:
        pl.semaphore_signal(barrier, inc=1, device_id={"dp": to}, device_id_type=pl.DeviceIdType.MESH)
    pl.semaphore_wait(barrier, len(WAYS))

    def halved(way):
        return range(way * layers // 2, (way + 1) * layers // 2)

    def slot(step, layer, way):
        return layer - halved(way)[0] if step == 1 else layers // 2 + (step - 2) * layers + layer

    def term_slot(step, layer, way):
        return layer - halved(way)[0] if step == 2 else layers // 2 + (step - 3) * layers + layer

    sums = {}

    def send_sum(way, step, layer, kind, src):
        here = slot(step, layer, way)
        sems = (rs_send.at[way, here, kind], rs_recv.at[way, here, kind])
        sums[way, step, layer, kind] = remote(src, got[kind].at[way, here], *sems, across[way])
        sums[way, step, layer, kind].start()

    for kind in range(kinds):
        for i in range(layers // 2):
            for way in range(2):
                layer = halved(way)[i]
                send_sum(way, 1, layer, kind, g[kind].at[layer, block(at(way, half), kind)])
    for kind in range(kinds):
        for i in range(layers // 2):
            for way in range(2):
                layer = halved(1 - way)[i]
                send_sum(way, 2, layer, kind, g[kind].at[layer, block(at(way, half - 1), kind)])

    loads = {}
    for step in range(2, half + 1):
        for way in range(2):
            first = halved(way)[0] if step == 2 else 0
            many = layers // 2 if step == 2 else layers
            for kind in range(kinds):
                src = g[kind].at[pl.ds(first, many), block(at(way, half + 1 - step), kind)]
                dst = term[kind].at[way, pl.ds(term_slot(step, first, way), many)]
                loads[way, step, kind] = pltpu.make_async_copy(src, dst, load_term.at[way, step - 2, kind])
                loads[way, step, kind].start()
    for kind in range(kinds):
        loads[kind] = pltpu.make_async_copy(g[kind].at[:, block(me, kind)], own[kind], load_own.at[kind])
        loads[kind].start()
    states = []
    for kind in range(kinds):
        here = block(me, kind)
        for which, (src, dst) in enumerate(
            ((m[kind], new_m[kind]), (v[kind], new_v[kind]), (w[kind].at[:, here], new_w[kind].at[:, here]))
        ):
            states.append(pltpu.make_async_copy(src, dst, load_state.at[which, kind]))
            states[-1].start()

    def each_rows(kind, body, carry=None):
        many = row_blocks(rows[kind], own[kind].shape[2])

        def one(i, carry):
            return body(pl.ds(pl.multiple_of(i * many, many), many), carry)

        return lax.fori_loop(0, rows[kind] // many, one, carry)

    def pass_on(way, step, layer, kind):
        sums[way, step - 1, layer, kind].wait_recv()
        into = got[kind].at[way, slot(step - 1, layer, way)]
        mine = term[kind].at[way, term_slot(step, layer, way)]

        def add(r, _):
            into[r] = (into[r].astype(jnp.float32) + mine[r].astype(jnp.float32)).astype(jnp.bfloat16)

        each_rows(kind, add)
        send_sum(way, step, layer, kind, into)

    waited = set()

    def loaded(*key):
        if key not in waited:
            waited.add(key)
            loads[key if len(key) > 1 else key[0]].wait()

    for kind in range(kinds):
        for i in range(layers // 2):
            for way in range(2):
                loaded(way, 2, kind)
                pass_on(way, 2, halved(way)[i], kind)
    for step in range(3, half + 1):
        for j in range(layers):
            for kind in range(kinds):
                for way in range(2):
                    order = (*halved(1 - way), *halved(way)) if step < half else range(layers)
                    loaded(way, step, kind)
                    pass_on(way, step, order[j], kind)

    total = jnp.zeros((8, 128), jnp.float32)
    for layer, kind in pairs:
        loaded(kind)
        for way in range(2):
            sums[way, half, layer, kind].wait_recv()
        ends = [got[kind].at[way, slot(half, layer, way)] for way in range(2)]
        mine = own[kind].at[layer]

        def finish(r, total):
            x = mine[r].astype(jnp.float32) + ends[0][r].astype(jnp.float32) + ends[1][r].astype(jnp.float32)
            x = x.astype(jnp.bfloat16)
            mine[r] = x
            x = x.astype(jnp.float32)
            x = x * x
            parts = [x[i : i + 8, j : j + 128] for i in range(0, x.shape[0], 8) for j in range(0, x.shape[1], 128)]
            while len(parts) > 1:
                parts = [a + b for a, b in zip(parts[::2], parts[1::2])] + ([parts[-1]] if len(parts) % 2 else [])
            return total + parts[0]

        total = each_rows(kind, finish, total)

    squares[me] = total
    told = []
    for off in range(1, n):
        sems = (sq_send.at[off - 1], sq_recv.at[off - 1])
        told.append(remote(squares.at[me], squares.at[me], *sems, lax.rem(me + off, n)))
        told[-1].start()
    for copy in states:
        copy.wait()
    for copy in told:
        copy.wait_recv()
    total = jnp.sum(squares[...], axis=0)
    total = jnp.sum(jnp.sum(total, axis=1, keepdims=True), axis=0, keepdims=True)
    factor = jnp.minimum(1.0, 0.5 * lax.rsqrt(total / count + 1e-30))

    gathers = {}

    def send_new(way, step, layer, kind):
        here = new_w[kind].at[layer, block(at(way, 1 - step), kind)]
        sems = (ag_send.at[way, step - 1, layer, kind], ag_recv.at[way, step - 1, layer, kind])
        gathers[way, step, layer, kind] = remote(here, here, *sems, across[way])
        gathers[way, step, layer, kind].start()

    for layer, kind in pairs:
        grad, m_at, v_at = own[kind].at[layer], new_m[kind].at[layer], new_v[kind].at[layer]
        base = pl.multiple_of(me * rows[kind], 16)
        w_at = new_w[kind].at[layer]

        def adamw(r, _):
            x = grad[r].astype(jnp.float32) * factor
            there = pl.ds(pl.multiple_of(base + r.start, 16), r.size)
            old = w_at[there].astype(jnp.float32)
            m_new = 0.9 * m_at[r] + 0.1 * x
            v_new = 0.95 * v_at[r] + 0.05 * x * x
            m_at[r] = m_new
            v_at[r] = v_new
            step = m_new * lax.rsqrt(v_new + 1e-8) + 0.1 * old
            w_at[there] = (old - 0.02 * step).astype(jnp.bfloat16)

        each_rows(kind, adamw)
        for way in range(2):
            send_new(way, 1, layer, kind)
    for step in range(1, half + 1):
        for layer, kind in pairs:
            for way in range(2):
                if step < half or layer in halved(way):
                    gathers[way, step, layer, kind].wait_recv()
                    if step < half - 1 or (step == half - 1 and layer in halved(way)):
                        send_new(way, step + 1, layer, kind)
    for copy in (*sums.values(), *told, *gathers.values()):
        copy.wait_send()


def solution(mesh):
    n = mesh.shape["dp"]

    def step(*arrays):
        terms, weights, m, v = (arrays[i : i + 3] for i in (0, 3, 6, 9))
        terms = [t[0] for t in terms]
        layers = m[0].shape[0]
        shapes = [one.shape[1:] for one in m]
        count = n * sum(one.size for one in m)
        half = n // 2
        sums = layers // 2 + (half - 1) * layers
        terms_kept = layers // 2 + (half - 2) * layers
        dma = pltpu.SemaphoreType.DMA
        scratch = [pltpu.VMEM((layers, *s), jnp.bfloat16) for s in shapes]
        scratch += [pltpu.VMEM((2, terms_kept, *s), jnp.bfloat16) for s in shapes]
        scratch += [pltpu.VMEM((2, sums, *s), jnp.bfloat16) for s in shapes]
        scratch += [pltpu.VMEM((n, 8, 128), jnp.float32)]
        scratch += [dma((2, sums, 3)), dma((2, sums, 3)), dma((2, half, layers, 3)), dma((2, half, layers, 3))]
        scratch += [dma((n - 1,)), dma((n - 1,)), dma((3,)), dma((2, half - 1, 3)), dma((3, 3))]
        out = [pltpu.VMEM(one.shape, one.dtype) for one in (*weights, *m, *v)]
        return pl.pallas_call(
            functools.partial(kernel, n, layers, count),
            out_shape=out,
            in_specs=[pl.BlockSpec(memory_space=pltpu.HBM)] * 12,
            out_specs=[pl.BlockSpec(memory_space=pltpu.VMEM)] * 9,
            scratch_shapes=scratch,
            compiler_params=pltpu.CompilerParams(collective_id=0, has_side_effects=True, vmem_limit_bytes=40 * 2**20),
        )(*terms, *weights, *m, *v)

    all_of, cut = P(None, None, None), P(None, "dp", None)
    return jax.shard_map(
        step,
        mesh=mesh,
        in_specs=(P(("rep", "dp"), None, None, None),) * 3 + (all_of,) * 3 + (cut,) * 6,
        out_specs=(P("rep", None, None),) * 3 + (P("rep", "dp", None),) * 6,
        check_vma=False,
    )
```

time: 354 us -> 250 us (0.71)
  waiting for transfers between devices: 295 us -> 0 us
  Pallas kernels: 0 us -> 238 us
  between operations: 16.9 us -> 0.66 us
  blocking collectives: 16.1 us -> 0 us
  other arithmetic: 14.8 us -> 0 us
    pallas_call x0 -> x1, Pallas kernels: none -> 238 us  [step(): pl.pallas_call(functools.partial(kernel, n, layers, count), out_shape=out...]
    reduce_scatter x3 -> x0, waiting for transfers between devices: 151 us -> none  [step(): lax.psum_scatter(t[0], 'dp', scatter_dimension=1, tiled=True)]
    all_gather x3 -> x0, waiting for transfers between devices: 141 us -> none  [step(): whole = [lax.all_gather(one[0], 'dp', axis=1, tiled=True) for one in new]]
    psum x1 -> x0, blocking collectives: 16.1 us -> none  [step(): squares = lax.psum(sum((jnp.sum(g * g) for g in gradients)), 'dp')]
    convert_element_type x3 -> x0, other arithmetic: 9.11 us -> none  [adamw(): return ((w - 0.02 * step).astype(jnp.bfloat16), m, v)]
    reduce_sum x3 -> x0, other arithmetic: 5.73 us -> none  [step(): squares = lax.psum(sum((jnp.sum(g * g) for g in gradients)), 'dp')]
    unnamed x19 -> x9, local copies, waits for them, and re-layouts: 9.93 us -> 11.4 us
  transfers between devices with their start and end apart: 6 -> 0, of which waited for: 6 -> 0; matrix products, arithmetic and copies ran while one was open for 3% -> 0% of each run, Pallas kernels for 0% -> 0%
where the time goes in v1:
time: 250 us
  Pallas kernels  238 us (95%)
  local copies, waits for them, and re-layouts  11.4 us (5%)
    pallas_call x1, Pallas kernels, step(): pl.pallas_call(functools.partial(kernel, n, layers, count), out_shape=out...  238 us
    unnamed x9, local copies, waits for them, and re-layouts  11.4 us

profile of v1, /device:TPU:22, one launch (start us, length us, event | category | flops | bytes accessed | tf_op | source)
XLA Modules:
  0.0 249.7 jit_solution(315581727348663829)
XLA Ops:
  0.6 237.7 %shard_map.187 = (bf16[2,640,1536]{2,1,0:T(8,128)(2,1)S(1)}, bf16[2,640,1536]{2,1,0:T(8,128)(2,1)S(1)}, bf16[2,1536,640]{2,1,0:T(8,128)(2,1)S(1)}, f32[2,80,1536...) custom-call(bf16[2,640,1536]{2,1,0:T(8,128)(2,1)} %bitcast.3, ...), custom_call_target="tpu_custom_call" | custom-call | tf_op jit(solution)/shard_map/pallas_call | solution.py:232
  238.3 1.9 copy.30
  240.2 0.9 copy.33
  241.2 0.9 copy.34
  242.1 0.9 copy.35
  243.1 0.9 copy.36
  244.0 0.9 copy.37
  245.0 0.9 copy.38
  245.9 1.9 copy.31
  247.8 1.9 copy.32

commit v2 on v1

--- a/solution.py
+++ b/solution.py
@@ -25,7 +25,7 @@
     new_w, new_m, new_v = (refs[i : i + kinds] for i in range(0, 3 * kinds, kinds))
     refs = refs[3 * kinds :]
     own, term, got = (refs[i : i + kinds] for i in range(0, 3 * kinds, kinds))
-    squares, rs_send, rs_recv, ag_send, ag_recv, sq_send, sq_recv, load_own, load_term, load_state = refs[3 * kinds :]
+    squares, arrived, rs_send, ag_send, sq_send, sq_recv, load_own, load_term, load_state = refs[3 * kinds :]
     half = n // 2
     me = lax.axis_index("dp")
     rows = [ref.shape[1] for ref in own]
@@ -60,10 +60,39 @@
 
     def send_sum(way, step, layer, kind, src):
         here = slot(step, layer, way)
-        sems = (rs_send.at[way, here, kind], rs_recv.at[way, here, kind])
+        sems = (rs_send.at[kind], arrived.at[way, here, kind])
         sums[way, step, layer, kind] = remote(src, got[kind].at[way, here], *sems, across[way])
         sums[way, step, layer, kind].start()
 
+    def fetch():
+        for kind in range(kinds):
+            for step in range(2, half + 1):
+                for way in range(2):
+                    first = halved(way)[0] if step == 2 else 0
+                    many = layers // 2 if step == 2 else layers
+                    src = g[kind].at[pl.ds(first, many), block(at(way, half + 1 - step), kind)]
+                    dst = term[kind].at[way, pl.ds(term_slot(step, first, way), many)]
+                    pltpu.make_async_copy(src, dst, load_term.at[kind]).start()
+        copies = []
+        for kind in range(kinds):
+            here = block(me, kind)
+            copies.append(pltpu.make_async_copy(g[kind].at[:, here], own[kind], load_own.at[kind]))
+            copies.append(pltpu.make_async_copy(m[kind], new_m[kind], load_state.at[0, kind]))
+            copies.append(pltpu.make_async_copy(v[kind], new_v[kind], load_state.at[1, kind]))
+            copies.append(pltpu.make_async_copy(w[kind].at[:, here], new_w[kind].at[:, here], load_state.at[2, kind]))
+        for copy in copies:
+            copy.start()
+        for kind in range(kinds):
+            pltpu.make_async_copy(term[kind], term[kind], load_term.at[kind]).wait()
+        for copy in copies:
+            copy.wait()
+
+    late = lax.rem(lax.axis_index("rep"), 2) == 0
+
+    @pl.when(late)
+    def _():
+        fetch()
+
     for kind in range(kinds):
         for i in range(layers // 2):
             for way in range(2):
@@ -75,27 +104,9 @@
                 layer = halved(1 - way)[i]
                 send_sum(way, 2, layer, kind, g[kind].at[layer, block(at(way, half - 1), kind)])
 
-    loads = {}
-    for step in range(2, half + 1):
-        for way in range(2):
-            first = halved(way)[0] if step == 2 else 0
-            many = layers // 2 if step == 2 else layers
-            for kind in range(kinds):
-                src = g[kind].at[pl.ds(first, many), block(at(way, half + 1 - step), kind)]
-                dst = term[kind].at[way, pl.ds(term_slot(step, first, way), many)]
-                loads[way, step, kind] = pltpu.make_async_copy(src, dst, load_term.at[way, step - 2, kind])
-                loads[way, step, kind].start()
-    for kind in range(kinds):
-        loads[kind] = pltpu.make_async_copy(g[kind].at[:, block(me, kind)], own[kind], load_own.at[kind])
-        loads[kind].start()
-    states = []
-    for kind in range(kinds):
-        here = block(me, kind)
-        for which, (src, dst) in enumerate(
-            ((m[kind], new_m[kind]), (v[kind], new_v[kind]), (w[kind].at[:, here], new_w[kind].at[:, here]))
-        ):
-            states.append(pltpu.make_async_copy(src, dst, load_state.at[which, kind]))
-            states[-1].start()
+    @pl.when(jnp.logical_not(late))
+    def _():
+        fetch()
 
     def each_rows(kind, body, carry=None):
         many = row_blocks(rows[kind], own[kind].shape[2])
@@ -116,29 +127,19 @@
         each_rows(kind, add)
         send_sum(way, step, layer, kind, into)
 
-    waited = set()
-
-    def loaded(*key):
-        if key not in waited:
-            waited.add(key)
-            loads[key if len(key) > 1 else key[0]].wait()
-
     for kind in range(kinds):
         for i in range(layers // 2):
             for way in range(2):
-                loaded(way, 2, kind)
                 pass_on(way, 2, halved(way)[i], kind)
     for step in range(3, half + 1):
         for j in range(layers):
             for kind in range(kinds):
                 for way in range(2):
                     order = (*halved(1 - way), *halved(way)) if step < half else range(layers)
-                    loaded(way, step, kind)
                     pass_on(way, step, order[j], kind)
 
     total = jnp.zeros((8, 128), jnp.float32)
     for layer, kind in pairs:
-        loaded(kind)
         for way in range(2):
             sums[way, half, layer, kind].wait_recv()
         ends = [got[kind].at[way, slot(half, layer, way)] for way in range(2)]
@@ -160,22 +161,22 @@
     squares[me] = total
     told = []
     for off in range(1, n):
-        sems = (sq_send.at[off - 1], sq_recv.at[off - 1])
-        told.append(remote(squares.at[me], squares.at[me], *sems, lax.rem(me + off, n)))
+        told.append(remote(squares.at[me], squares.at[me], sq_send.at[0], sq_recv.at[0], lax.rem(me + off, n)))
         told[-1].start()
-    for copy in states:
-        copy.wait()
-    for copy in told:
-        copy.wait_recv()
+    others = squares.at[pl.ds(0, n - 1)]
+    pltpu.make_async_copy(others, others, sq_recv.at[0]).wait()
     total = jnp.sum(squares[...], axis=0)
     total = jnp.sum(jnp.sum(total, axis=1, keepdims=True), axis=0, keepdims=True)
     factor = jnp.minimum(1.0, 0.5 * lax.rsqrt(total / count + 1e-30))
 
     gathers = {}
 
+    def gather_slot(way, step, layer):
+        return (step - 1) * layers + (layer if step < half else layer - halved(way)[0])
+
     def send_new(way, step, layer, kind):
         here = new_w[kind].at[layer, block(at(way, 1 - step), kind)]
-        sems = (ag_send.at[way, step - 1, layer, kind], ag_recv.at[way, step - 1, layer, kind])
+        sems = (ag_send.at[kind], arrived.at[way, gather_slot(way, step, layer), kind])
         gathers[way, step, layer, kind] = remote(here, here, *sems, across[way])
         gathers[way, step, layer, kind].start()
 
@@ -205,8 +206,19 @@
                     gathers[way, step, layer, kind].wait_recv()
                     if step < half - 1 or (step == half - 1 and layer in halved(way)):
                         send_new(way, step + 1, layer, kind)
-    for copy in (*sums.values(), *told, *gathers.values()):
-        copy.wait_send()
+    for kind in range(kinds):
+        for sem in (rs_send, ag_send):
+            pltpu.make_async_copy(got[kind], got[kind], sem.at[kind]).wait()
+    pltpu.make_async_copy(others, others, sq_send.at[0]).wait()
+
+
+def write_out(*refs):
+    n = (len(refs) - 1) // 2
+    copies = [pltpu.make_async_copy(src, dst, refs[-1].at[i]) for i, (src, dst) in enumerate(zip(refs[:n], refs[n : 2 * n]))]
+    for copy in copies:
+        copy.start()
+    for copy in copies:
+        copy.wait()
 
 
 def solution(mesh):
@@ -226,10 +238,9 @@
         scratch += [pltpu.VMEM((2, terms_kept, *s), jnp.bfloat16) for s in shapes]
         scratch += [pltpu.VMEM((2, sums, *s), jnp.bfloat16) for s in shapes]
         scratch += [pltpu.VMEM((n, 8, 128), jnp.float32)]
-        scratch += [dma((2, sums, 3)), dma((2, sums, 3)), dma((2, half, layers, 3)), dma((2, half, layers, 3))]
-        scratch += [dma((n - 1,)), dma((n - 1,)), dma((3,)), dma((2, half - 1, 3)), dma((3, 3))]
+        scratch += [dma((2, sums, 3)), dma((3,)), dma((3,)), dma((1,)), dma((1,)), dma((3,)), dma((3,)), dma((3, 3))]
         out = [pltpu.VMEM(one.shape, one.dtype) for one in (*weights, *m, *v)]
-        return pl.pallas_call(
+        kept = pl.pallas_call(
             functools.partial(kernel, n, layers, count),
             out_shape=out,
             in_specs=[pl.BlockSpec(memory_space=pltpu.HBM)] * 12,
@@ -237,6 +248,14 @@
             scratch_shapes=scratch,
             compiler_params=pltpu.CompilerParams(collective_id=0, has_side_effects=True, vmem_limit_bytes=40 * 2**20),
         )(*terms, *weights, *m, *v)
+        return pl.pallas_call(
+            write_out,
+            out_shape=[jax.ShapeDtypeStruct(one.shape, one.dtype) for one in kept],
+            in_specs=[pl.BlockSpec(memory_space=pltpu.VMEM)] * 9,
+            out_specs=[pl.BlockSpec(memory_space=pltpu.HBM)] * 9,
+            scratch_shapes=[dma((9,))],
+            compiler_params=pltpu.CompilerParams(vmem_limit_bytes=2**20),
+        )(*kept)
 
     all_of, cut = P(None, None, None), P(None, "dp", None)
     return jax.shard_map(

time: 250 us -> 238 us (0.952)
  local copies, waits for them, and re-layouts: 11.4 us -> 0 us
    unnamed x9 -> x0, local copies, waits for them, and re-layouts: 11.4 us -> none
    pallas_call x1, Pallas kernels: 238 us -> 231 us  [step(): pl.pallas_call(functools.partial(kernel, n, layers, count), out_shape=out...]
    pallas_call x0 -> x1, Pallas kernels: none -> 6.28 us  [step(): pl.pallas_call(write_out, out_shape=[jax.ShapeDtypeStruct(one.shape, one....]
where the time goes in v2:
time: 238 us
  Pallas kernels  237 us (100%)
    pallas_call x1, Pallas kernels, step(): pl.pallas_call(functools.partial(kernel, n, layers, count), out_shape=out...  231 us
    pallas_call x1, Pallas kernels, step(): pl.pallas_call(write_out, out_shape=[jax.ShapeDtypeStruct(one.shape, one....  6.28 us

profile of v2, /device:TPU:22, one launch (start us, length us, event | category | flops | bytes accessed | tf_op | source)
XLA Modules:
  0.0 238.1 jit_solution(2752984984001959846)
XLA Ops:
  0.6 231.1 %shard_map.187 = (bf16[2,640,1536]{2,1,0:T(8,128)(2,1)S(1)}, bf16[2,640,1536]{2,1,0:T(8,128)(2,1)S(1)}, bf16[2,1536,640]{2,1,0:T(8,128)(2,1)S(1)}, f32[2,80,1536...) custom-call(bf16[2,640,1536]{2,1,0:T(8,128)(2,1)} %bitcast.3, ...), custom_call_target="tpu_custom_call" | custom-call | tf_op jit(solution)/shard_map/pallas_call | solution.py:243
  231.8 6.3 %shard_map.188 = (bf16[2,640,1536]{2,1,0:T(8,128)(2,1)}, bf16[2,640,1536]{2,1,0:T(8,128)(2,1)}, bf16[2,1536,640]{2,1,0:T(8,128)(2,1)}, f32[2,80,1536]{2,1,0:T(8,...) custom-call(bf16[2,640,1536]{2,1,0:T(8,128)(2,1)S(1)} %get-tuple-ele, ...), custom_call_target="tpu_custom_call" | custom-call | tf_op jit(solution)/shard_map/pallas_call | solution.py:251

commit v3 on v2

v3 whole, which is shorter than its diff:
```python
import functools

import jax
import jax.numpy as jnp
from jax import lax
from jax.experimental import pallas as pl
from jax.experimental.pallas import tpu as pltpu
from jax.sharding import PartitionSpec as P

WAYS = (1, -1)
LAG_NS = 5000


def row_blocks(rows, columns):
    best = 16
    for step in range(16, rows + 1, 16):
        if rows % step == 0 and step * columns <= 32 * 1024:
            best = step
    return best


def remote(src, dst, send, recv, to):
    return pltpu.make_async_remote_copy(src, dst, send, recv, device_id={"dp": to}, device_id_type=pl.DeviceIdType.MESH)


def meet(n):
    me = lax.axis_index("dp")

    def at(way, steps):
        return lax.rem(me + WAYS[way] * steps + n, n)

    barrier = pltpu.get_barrier_semaphore()
    for way in range(2):
        pl.semaphore_signal(barrier, inc=1, device_id={"dp": at(way, 1)}, device_id_type=pl.DeviceIdType.MESH)
    pl.semaphore_wait(barrier, 2)
    return me, at


def halved(layers, way):
    return range(way * layers // 2, (way + 1) * layers // 2)


class Gather:
    def __init__(self, n, at, outs, rows, arrived, sent):
        self.half, self.at, self.outs, self.rows, self.arrived, self.sent = n // 2, at, outs, rows, arrived, sent
        self.n, self.layers, self.copies = n, outs[0].shape[0], {}

    def block(self, chunk, kind):
        return pl.ds(pl.multiple_of(chunk * self.rows[kind], 16), self.rows[kind])

    def send(self, way, step, layer, kind, src=None):
        here = self.outs[kind].at[layer, self.block(self.at(way, 1 - step), kind)]
        slot = (step - 1) * self.layers + (layer if step < self.half else layer - halved(self.layers, way)[0])
        copy = remote(here if src is None else src, here, self.sent.at[kind], self.arrived.at[way, slot, kind], self.at(way, 1))
        self.copies[way, step, layer, kind] = copy
        copy.start()

    def run(self):
        for step in range(1, self.half + 1):
            for i in range(self.layers):
                for kind in range(len(self.outs)):
                    for way in range(2):
                        far = halved(self.layers, way)
                        layer = (*far, *halved(self.layers, 1 - way))[i]
                        if step == self.half and layer not in far:
                            continue
                        self.copies[way, step, layer, kind].wait_recv()
                        if step < self.half - 1 or (step == self.half - 1 and layer in far):
                            self.send(way, step + 1, layer, kind)
        for kind, out in enumerate(self.outs):
            moved = out.at[:, pl.ds(0, (self.n - 1) * self.rows[kind])]
            pltpu.make_async_copy(moved, moved, self.sent.at[kind]).wait()


def sum_and_step(n, layers, count, *refs):
    kinds = 3
    g, w, m, v = (refs[i : i + kinds] for i in range(0, 4 * kinds, kinds))
    refs = refs[4 * kinds :]
    new_w, new_m, new_v = (refs[i : i + kinds] for i in range(0, 3 * kinds, kinds))
    refs = refs[3 * kinds :]
    own, term, got = (refs[i : i + kinds] for i in range(0, 3 * kinds, kinds))
    squares, arrived, rs_send, ag_send, sq_send, sq_recv, load_own, load_term, load_state = refs[3 * kinds :]
    half = n // 2
    rows = [ref.shape[1] for ref in own]
    pairs = [(layer, kind) for kind in range(kinds) for layer in range(layers)]
    me, at = meet(n)

    def block(chunk, kind):
        return pl.ds(pl.multiple_of(chunk * rows[kind], 16), rows[kind])

    def slot(step, layer, way):
        return layer - halved(layers, way)[0] if step == 1 else layers // 2 + (step - 2) * layers + layer

    def term_slot(step, layer, way):
        return layer - halved(layers, way)[0] if step == 2 else layers // 2 + (step - 3) * layers + layer

    sums = {}

    def send_sum(way, step, layer, kind, src):
        here = slot(step, layer, way)
        sems = (rs_send.at[kind], arrived.at[way, here, kind])
        sums[way, step, layer, kind] = remote(src, got[kind].at[way, here], *sems, at(way, 1))
        sums[way, step, layer, kind].start()

    def fetch():
        for kind in range(kinds):
            for step in range(2, half + 1):
                for way in range(2):
                    first = halved(layers, way)[0] if step == 2 else 0
                    many = layers // 2 if step == 2 else layers
                    src = g[kind].at[pl.ds(first, many), block(at(way, half + 1 - step), kind)]
                    dst = term[kind].at[way, pl.ds(term_slot(step, first, way), many)]
                    pltpu.make_async_copy(src, dst, load_term.at[kind]).start()
        copies = []
        for kind in range(kinds):
            here = block(me, kind)
            copies.append(pltpu.make_async_copy(g[kind].at[:, here], own[kind], load_own.at[kind]))
            copies.append(pltpu.make_async_copy(m[kind], new_m[kind], load_state.at[0, kind]))
            copies.append(pltpu.make_async_copy(v[kind], new_v[kind], load_state.at[1, kind]))
            to = new_w[kind].at[:, here] if kind < kinds - 1 else new_w[kind]
            copies.append(pltpu.make_async_copy(w[kind].at[:, here], to, load_state.at[2, kind]))
        for copy in copies:
            copy.start()
        for kind in range(kinds):
            pltpu.make_async_copy(term[kind], term[kind], load_term.at[kind]).wait()
        for copy in copies:
            copy.wait()

    late = lax.rem(lax.axis_index("rep"), 2) == 0

    @pl.when(late)
    def _():
        fetch()
        pl.delay(LAG_NS)

    for kind in range(kinds):
        for i in range(layers // 2):
            for way in range(2):
                layer = halved(layers, way)[i]
                send_sum(way, 1, layer, kind, g[kind].at[layer, block(at(way, half), kind)])
    for kind in range(kinds):
        for i in range(layers // 2):
            for way in range(2):
                layer = halved(layers, 1 - way)[i]
                send_sum(way, 2, layer, kind, g[kind].at[layer, block(at(way, half - 1), kind)])

    @pl.when(jnp.logical_not(late))
    def _():
        fetch()

    def each_rows(kind, body, carry=None):
        many = row_blocks(rows[kind], own[kind].shape[2])

        def one(i, carry):
            return body(pl.ds(pl.multiple_of(i * many, many), many), carry)

        return lax.fori_loop(0, rows[kind] // many, one, carry)

    def pass_on(way, step, layer, kind):
        sums[way, step - 1, layer, kind].wait_recv()
        into = got[kind].at[way, slot(step - 1, layer, way)]
        mine = term[kind].at[way, term_slot(step, layer, way)]

        def add(r, _):
            into[r] = (into[r].astype(jnp.float32) + mine[r].astype(jnp.float32)).astype(jnp.bfloat16)

        each_rows(kind, add)
        send_sum(way, step, layer, kind, into)

    for kind in range(kinds):
        for i in range(layers // 2):
            for way in range(2):
                pass_on(way, 2, halved(layers, way)[i], kind)
    for step in range(3, half + 1):
        for j in range(layers):
            for kind in range(kinds):
                for way in range(2):
                    order = (*halved(layers, 1 - way), *halved(layers, way)) if step < half else range(layers)
                    pass_on(way, step, order[j], kind)

    total = jnp.zeros((8, 128), jnp.float32)
    for layer, kind in pairs:
        for way in range(2):
            sums[way, half, layer, kind].wait_recv()
        ends = [got[kind].at[way, slot(half, layer, way)] for way in range(2)]
        mine = own[kind].at[layer]

        def finish(r, total):
            x = mine[r].astype(jnp.float32) + ends[0][r].astype(jnp.float32) + ends[1][r].astype(jnp.float32)
            x = x.astype(jnp.bfloat16)
            mine[r] = x
            x = x.astype(jnp.float32)
            x = x * x
            parts = [x[i : i + 8, j : j + 128] for i in range(0, x.shape[0], 8) for j in range(0, x.shape[1], 128)]
            while len(parts) > 1:
                parts = [a + b for a, b in zip(parts[::2], parts[1::2])] + ([parts[-1]] if len(parts) % 2 else [])
            return total + parts[0]

        total = each_rows(kind, finish, total)

    squares[me] = total
    told = []
    for off in range(1, n):
        told.append(remote(squares.at[me], squares.at[me], sq_send.at[0], sq_recv.at[0], lax.rem(me + off, n)))
        told[-1].start()
    others = squares.at[pl.ds(0, n - 1)]
    pltpu.make_async_copy(others, others, sq_recv.at[0]).wait()
    total = jnp.sum(squares[...], axis=0)
    total = jnp.sum(jnp.sum(total, axis=1, keepdims=True), axis=0, keepdims=True)
    factor = jnp.minimum(1.0, 0.5 * lax.rsqrt(total / count + 1e-30))

    gather = Gather(n, at, new_w[: kinds - 1], rows, arrived, ag_send)
    for kind in range(kinds):
        for layer in range(layers):
            grad, m_at, v_at = own[kind].at[layer], new_m[kind].at[layer], new_v[kind].at[layer]
            base = pl.multiple_of(me * rows[kind], 16) if kind < kinds - 1 else 0
            w_at = new_w[kind].at[layer]

            def adamw(r, _):
                x = grad[r].astype(jnp.float32) * factor
                there = pl.ds(pl.multiple_of(base + r.start, 16), r.size)
                old = w_at[there].astype(jnp.float32)
                m_new = 0.9 * m_at[r] + 0.1 * x
                v_new = 0.95 * v_at[r] + 0.05 * x * x
                m_at[r] = m_new
                v_at[r] = v_new
                step = m_new * lax.rsqrt(v_new + 1e-8) + 0.1 * old
                w_at[there] = (old - 0.02 * step).astype(jnp.bfloat16)

            each_rows(kind, adamw)
            if kind < kinds - 1:
                for way in range(2):
                    gather.send(way, 1, layer, kind)
    gather.run()
    for kind in range(kinds):
        pltpu.make_async_copy(got[kind], got[kind], rs_send.at[kind]).wait()
    pltpu.make_async_copy(others, others, sq_send.at[0]).wait()


def gather_last(n, own, after, out, arrived, sent):
    me, at = meet(n)
    gather = Gather(n, at, [out], [own.shape[1]], arrived, sent)
    for i in range(own.shape[0]):
        for way in range(2):
            layer = (*halved(own.shape[0], way), *halved(own.shape[0], 1 - way))[i]
            gather.send(way, 1, layer, 0, own.at[layer])
    out[:, gather.block(me, 0)] = own[...]
    gather.run()


def write_out(*refs):
    n = (len(refs) - 2) // 2
    copies = [pltpu.make_async_copy(src, dst, refs[-1].at[i]) for i, (src, dst) in enumerate(zip(refs[:n], refs[n : 2 * n]))]
    refs[-2][...] = jnp.zeros_like(refs[-2])
    for copy in copies:
        copy.start()
    for copy in copies:
        copy.wait()


def solution(mesh):
    n = mesh.shape["dp"]

    def step(*arrays):
        terms, weights, m, v = (arrays[i : i + 3] for i in (0, 3, 6, 9))
        terms = [t[0] for t in terms]
        layers = m[0].shape[0]
        shapes = [one.shape[1:] for one in m]
        count = n * sum(one.size for one in m)
        half = n // 2
        sums = layers // 2 + (half - 1) * layers
        terms_kept = layers // 2 + (half - 2) * layers
        dma = pltpu.SemaphoreType.DMA
        scratch = [pltpu.VMEM((layers, *s), jnp.bfloat16) for s in shapes]
        scratch += [pltpu.VMEM((2, terms_kept, *s), jnp.bfloat16) for s in shapes]
        scratch += [pltpu.VMEM((2, sums, *s), jnp.bfloat16) for s in shapes]
        scratch += [pltpu.VMEM((n, 8, 128), jnp.float32)]
        scratch += [dma((2, sums, 3)), dma((3,)), dma((2,)), dma((1,)), dma((1,)), dma((3,)), dma((3,)), dma((3, 3))]
        in_vmem, in_hbm = pl.BlockSpec(memory_space=pltpu.VMEM), pl.BlockSpec(memory_space=pltpu.HBM)
        new = [*weights[:2], jax.ShapeDtypeStruct(m[2].shape, weights[2].dtype), *m, *v]
        new = pl.pallas_call(
            functools.partial(sum_and_step, n, layers, count),
            out_shape=[pltpu.VMEM(one.shape, one.dtype) for one in new],
            in_specs=[in_hbm] * 12,
            out_specs=[in_vmem] * 9,
            scratch_shapes=scratch,
            compiler_params=pltpu.CompilerParams(collective_id=0, has_side_effects=True, vmem_limit_bytes=40 * 2**20),
        )(*terms, *weights, *m, *v)

        def written(*kept):
            return pl.pallas_call(
                write_out,
                out_shape=[*(jax.ShapeDtypeStruct(one.shape, one.dtype) for one in kept), pltpu.VMEM((8, 128), jnp.float32)],
                in_specs=[in_vmem] * len(kept),
                out_specs=[in_hbm] * len(kept) + [in_vmem],
                scratch_shapes=[dma((len(kept),))],
                compiler_params=pltpu.CompilerParams(vmem_limit_bytes=2**20),
            )(*kept)

        gate, up, *moments, done = written(*new[:2], *new[3:])
        down = pl.pallas_call(
            functools.partial(gather_last, n),
            out_shape=pltpu.VMEM(weights[2].shape, weights[2].dtype),
            in_specs=[in_vmem, in_vmem],
            out_specs=in_vmem,
            scratch_shapes=[dma((2, sums, 1)), dma((1,))],
            compiler_params=pltpu.CompilerParams(collective_id=1, has_side_effects=True, vmem_limit_bytes=2**20),
        )(new[2], done)
        return (gate, up, down, *moments)

    all_of, cut = P(None, None, None), P(None, "dp", None)
    return jax.shard_map(
        step,
        mesh=mesh,
        in_specs=(P(("rep", "dp"), None, None, None),) * 3 + (all_of,) * 3 + (cut,) * 6,
        out_specs=(P("rep", None, None),) * 3 + (P("rep", "dp", None),) * 6,
        check_vma=False,
    )
```

time: 238 us -> 233 us (0.979)
  Pallas kernels: 237 us -> 231 us
    pallas_call x2 -> x3, Pallas kernels: 237 us -> 231 us  [the longest x1 197 us: step(): pl.pallas_call(functools.partial(sum_and_step, n, layers, count), out_sha...]
where the time goes in v3:
time: 233 us
  Pallas kernels  231 us (99%)
    pallas_call x1, Pallas kernels, step(): pl.pallas_call(functools.partial(sum_and_step, n, layers, count), out_sha...  197 us
    pallas_call x1, Pallas kernels, step(): pl.pallas_call(functools.partial(gather_last, n), out_shape=pltpu.VMEM(we...  28.4 us
    pallas_call x1, Pallas kernels, written(): pl.pallas_call(write_out, out_shape=[*(jax.ShapeDtypeStruct(one.shape, on...  5.09 us

profile of v3, /device:TPU:22, one launch (start us, length us, event | category | flops | bytes accessed | tf_op | source)
XLA Modules:
  0.0 233.4 jit_solution(909484273953256158)
XLA Ops:
  0.6 197.3 %shard_map.187 = (bf16[2,640,1536]{2,1,0:T(8,128)(2,1)S(1)}, bf16[2,640,1536]{2,1,0:T(8,128)(2,1)S(1)}, bf16[2,192,640]{2,1,0:T(8,128)(2,1)S(1)}, f32[2,80,1536]...) custom-call(bf16[2,640,1536]{2,1,0:T(8,128)(2,1)} %bitcast.3, ...), custom_call_target="tpu_custom_call" | custom-call | tf_op jit(solution)/shard_map/pallas_call | solution.py:281
  197.9 5.1 %shard_map.188 = (bf16[2,640,1536]{2,1,0:T(8,128)(2,1)}, bf16[2,640,1536]{2,1,0:T(8,128)(2,1)}, f32[2,80,1536]{2,1,0:T(8,128)}, f32[2,80,1536]{2,1,0:T(8,128)}, ...) custom-call(bf16[2,640,1536]{2,1,0:T(8,128)(2,1)S(1)} %get-tuple-ele, ...), custom_call_target="tpu_custom_call" | custom-call | tf_op jit(solution)/shard_map/pallas_call | solution.py:291
  203.0 28.4 %shard_map.189 = bf16[2,1536,640]{2,1,0:T(8,128)(2,1)S(1)} custom-call(bf16[2,192,640]{2,1,0:T(8,128)(2,1)S(1)} %get-tuple-element.37.own, f32[8,128]{1,0:T(8,128)S(1)} %get-tuple-element.38.after), custom_call_target="tpu_custom_call" | custom-call | tf_op jit(solution)/shard_map/pallas_call | solution.py:301
  231.5 1.9 copy.22

commit v4 on v3

--- a/solution.py
+++ b/solution.py
@@ -8,7 +8,7 @@
 from jax.sharding import PartitionSpec as P
 
 WAYS = (1, -1)
-LAG_NS = 5000
+LAG_NS = 6000
 
 
 def row_blocks(rows, columns):
@@ -198,15 +198,14 @@
 
         total = each_rows(kind, finish, total)
 
-    squares[me] = total
+    squares[me] = jnp.sum(total, axis=0, keepdims=True)
     told = []
     for off in range(1, n):
         told.append(remote(squares.at[me], squares.at[me], sq_send.at[0], sq_recv.at[0], lax.rem(me + off, n)))
         told[-1].start()
     others = squares.at[pl.ds(0, n - 1)]
     pltpu.make_async_copy(others, others, sq_recv.at[0]).wait()
-    total = jnp.sum(squares[...], axis=0)
-    total = jnp.sum(jnp.sum(total, axis=1, keepdims=True), axis=0, keepdims=True)
+    total = jnp.sum(jnp.sum(squares[...], axis=0), axis=1, keepdims=True)
     factor = jnp.minimum(1.0, 0.5 * lax.rsqrt(total / count + 1e-30))
 
     gather = Gather(n, at, new_w[: kinds - 1], rows, arrived, ag_send)
@@ -274,7 +273,7 @@
         scratch = [pltpu.VMEM((layers, *s), jnp.bfloat16) for s in shapes]
         scratch += [pltpu.VMEM((2, terms_kept, *s), jnp.bfloat16) for s in shapes]
         scratch += [pltpu.VMEM((2, sums, *s), jnp.bfloat16) for s in shapes]
-        scratch += [pltpu.VMEM((n, 8, 128), jnp.float32)]
+        scratch += [pltpu.VMEM((n, 1, 128), jnp.float32)]
         scratch += [dma((2, sums, 3)), dma((3,)), dma((2,)), dma((1,)), dma((1,)), dma((3,)), dma((3,)), dma((3, 3))]
         in_vmem, in_hbm = pl.BlockSpec(memory_space=pltpu.VMEM), pl.BlockSpec(memory_space=pltpu.HBM)
         new = [*weights[:2], jax.ShapeDtypeStruct(m[2].shape, weights[2].dtype), *m, *v]

time: 233 us -> 233 us (level)
  no operation moved by 1% of the time
where the time goes in v4:
time: 233 us
  Pallas kernels  230 us (99%)
    pallas_call x1, Pallas kernels, step(): pl.pallas_call(functools.partial(sum_and_step, n, layers, count), out_sha...  198 us
    pallas_call x1, Pallas kernels, step(): pl.pallas_call(functools.partial(gather_last, n), out_shape=pltpu.VMEM(we...  27.3 us
    pallas_call x1, Pallas kernels, written(): pl.pallas_call(write_out, out_shape=[*(jax.ShapeDtypeStruct(one.shape, on...  5.09 us

profile of v4, /device:TPU:22, one launch (start us, length us, event | category | flops | bytes accessed | tf_op | source)
XLA Modules:
  0.0 232.9 jit_solution(4496485107843593996)
XLA Ops:
  0.6 197.9 %shard_map.187 = (bf16[2,640,1536]{2,1,0:T(8,128)(2,1)S(1)}, bf16[2,640,1536]{2,1,0:T(8,128)(2,1)S(1)}, bf16[2,192,640]{2,1,0:T(8,128)(2,1)S(1)}, f32[2,80,1536]...) custom-call(bf16[2,640,1536]{2,1,0:T(8,128)(2,1)} %bitcast.3, ...), custom_call_target="tpu_custom_call" | custom-call | tf_op jit(solution)/shard_map/pallas_call | solution.py:280
  198.6 5.1 %shard_map.188 = (bf16[2,640,1536]{2,1,0:T(8,128)(2,1)}, bf16[2,640,1536]{2,1,0:T(8,128)(2,1)}, f32[2,80,1536]{2,1,0:T(8,128)}, f32[2,80,1536]{2,1,0:T(8,128)}, ...) custom-call(bf16[2,640,1536]{2,1,0:T(8,128)(2,1)S(1)} %get-tuple-ele, ...), custom_call_target="tpu_custom_call" | custom-call | tf_op jit(solution)/shard_map/pallas_call | solution.py:290
  203.7 27.3 %shard_map.189 = bf16[2,1536,640]{2,1,0:T(8,128)(2,1)S(1)} custom-call(bf16[2,192,640]{2,1,0:T(8,128)(2,1)S(1)} %get-tuple-element.37.own, f32[8,128]{1,0:T(8,128)S(1)} %get-tuple-element.38.after), custom_call_target="tpu_custom_call" | custom-call | tf_op jit(solution)/shard_map/pallas_call | solution.py:300
  231.0 1.9 copy.22

commit v5 on v4

--- a/solution.py
+++ b/solution.py
@@ -8,7 +8,8 @@
 from jax.sharding import PartitionSpec as P
 
 WAYS = (1, -1)
-LAG_NS = 6000
+LAG_NS = 4000
+PAUSE_NS = 11700
 
 
 def row_blocks(rows, columns):
@@ -23,53 +24,57 @@
     return pltpu.make_async_remote_copy(src, dst, send, recv, device_id={"dp": to}, device_id_type=pl.DeviceIdType.MESH)
 
 
-def meet(n):
+def ring(n):
     me = lax.axis_index("dp")
-
-    def at(way, steps):
-        return lax.rem(me + WAYS[way] * steps + n, n)
-
+    return me, lambda way, steps: lax.rem(me + WAYS[way] * steps + n, n)
+
+
+def meet(at):
     barrier = pltpu.get_barrier_semaphore()
     for way in range(2):
         pl.semaphore_signal(barrier, inc=1, device_id={"dp": at(way, 1)}, device_id_type=pl.DeviceIdType.MESH)
     pl.semaphore_wait(barrier, 2)
-    return me, at
 
 
 def halved(layers, way):
     return range(way * layers // 2, (way + 1) * layers // 2)
 
 
+def ends_last():
+    return lax.rem(lax.axis_index("rep"), 2) == 0
+
+
 class Gather:
-    def __init__(self, n, at, outs, rows, arrived, sent):
-        self.half, self.at, self.outs, self.rows, self.arrived, self.sent = n // 2, at, outs, rows, arrived, sent
-        self.n, self.layers, self.copies = n, outs[0].shape[0], {}
-
-    def block(self, chunk, kind):
-        return pl.ds(pl.multiple_of(chunk * self.rows[kind], 16), self.rows[kind])
-
-    def send(self, way, step, layer, kind, src=None):
-        here = self.outs[kind].at[layer, self.block(self.at(way, 1 - step), kind)]
-        slot = (step - 1) * self.layers + (layer if step < self.half else layer - halved(self.layers, way)[0])
-        copy = remote(here if src is None else src, here, self.sent.at[kind], self.arrived.at[way, slot, kind], self.at(way, 1))
-        self.copies[way, step, layer, kind] = copy
-        copy.start()
-
-    def run(self):
+    def __init__(self, n, at, outs, rows, orders, arrived, sent):
+        self.n, self.half, self.at, self.outs, self.rows, self.orders = n, n // 2, at, outs, rows, orders
+        self.arrived, self.sent = arrived, sent
+
+    def order(self, way, step):
+        return [piece for piece in self.orders[way] if step < self.half or piece[4] == way]
+
+    def copy(self, way, step, piece, src=None):
+        kind, layer, first, many, _ = piece
+        here = self.outs[kind].at[layer, pl.ds(pl.multiple_of(self.at(way, 1 - step) * self.rows[kind] + first, 16), many)]
+        arrived = self.arrived.at[way, (step - 1) * len(self.orders[way]) + self.order(way, step).index(piece)]
+        return remote(here if src is None else src, here, self.sent.at[kind], arrived, self.at(way, 1))
+
+    def run(self, short=()):
         for step in range(1, self.half + 1):
-            for i in range(self.layers):
-                for kind in range(len(self.outs)):
-                    for way in range(2):
-                        far = halved(self.layers, way)
-                        layer = (*far, *halved(self.layers, 1 - way))[i]
-                        if step == self.half and layer not in far:
+            for i in range(len(self.orders[0])):
+                for way in range(2):
+                    for piece in self.order(way, step)[i : i + 1]:
+                        if step == self.half and piece[0] in short:
                             continue
-                        self.copies[way, step, layer, kind].wait_recv()
-                        if step < self.half - 1 or (step == self.half - 1 and layer in far):
-                            self.send(way, step + 1, layer, kind)
-        for kind, out in enumerate(self.outs):
-            moved = out.at[:, pl.ds(0, (self.n - 1) * self.rows[kind])]
-            pltpu.make_async_copy(moved, moved, self.sent.at[kind]).wait()
+                        self.copy(way, step, piece).wait_recv()
+                        if step < self.half and piece in self.order(way, step + 1) and not (step + 1 == self.half and piece[0] in short):
+                            self.copy(way, step + 1, piece).start()
+        for kind in sorted({piece[0] for piece in self.orders[0]}):
+            blocks = self.n - 2 if kind in short else self.n - 1
+            self.wait_sent(kind, blocks)
+
+    def wait_sent(self, kind, blocks):
+        moved = self.outs[kind].at[:, pl.ds(0, blocks * self.rows[kind])]
+        pltpu.make_async_copy(moved, moved, self.sent.at[kind]).wait()
 
 
 def sum_and_step(n, layers, count, *refs):
@@ -83,7 +88,8 @@
     half = n // 2
     rows = [ref.shape[1] for ref in own]
     pairs = [(layer, kind) for kind in range(kinds) for layer in range(layers)]
-    me, at = meet(n)
+    me, at = ring(n)
+    meet(at)
 
     def block(chunk, kind):
         return pl.ds(pl.multiple_of(chunk * rows[kind], 16), rows[kind])
@@ -98,7 +104,7 @@
 
     def send_sum(way, step, layer, kind, src):
         here = slot(step, layer, way)
-        sems = (rs_send.at[kind], arrived.at[way, here, kind])
+        sems = (rs_send.at[kind], arrived.at[way, here * kinds + kind])
         sums[way, step, layer, kind] = remote(src, got[kind].at[way, here], *sems, at(way, 1))
         sums[way, step, layer, kind].start()
 
@@ -117,8 +123,7 @@
             copies.append(pltpu.make_async_copy(g[kind].at[:, here], own[kind], load_own.at[kind]))
             copies.append(pltpu.make_async_copy(m[kind], new_m[kind], load_state.at[0, kind]))
             copies.append(pltpu.make_async_copy(v[kind], new_v[kind], load_state.at[1, kind]))
-            to = new_w[kind].at[:, here] if kind < kinds - 1 else new_w[kind]
-            copies.append(pltpu.make_async_copy(w[kind].at[:, here], to, load_state.at[2, kind]))
+            copies.append(pltpu.make_async_copy(w[kind].at[:, here], new_w[kind].at[:, here], load_state.at[2, kind]))
         for copy in copies:
             copy.start()
         for kind in range(kinds):
@@ -126,7 +131,7 @@
         for copy in copies:
             copy.wait()
 
-    late = lax.rem(lax.axis_index("rep"), 2) == 0
+    late = ends_last()
 
     @pl.when(late)
     def _():
@@ -208,11 +213,13 @@
     total = jnp.sum(jnp.sum(squares[...], axis=0), axis=1, keepdims=True)
     factor = jnp.minimum(1.0, 0.5 * lax.rsqrt(total / count + 1e-30))
 
-    gather = Gather(n, at, new_w[: kinds - 1], rows, arrived, ag_send)
+    pieces = [[(kind, layer, 0, rows[kind], layer * 2 // layers) for kind in range(kinds)] for layer in range(layers)]
+    some = Gather(n, at, new_w, rows, [sum((one[:-1] for one in pieces[::step]), []) for step in WAYS], arrived, ag_send)
+    more = Gather(n, at, new_w, rows, [sum(pieces[::step], []) for step in WAYS], arrived, ag_send)
     for kind in range(kinds):
         for layer in range(layers):
             grad, m_at, v_at = own[kind].at[layer], new_m[kind].at[layer], new_v[kind].at[layer]
-            base = pl.multiple_of(me * rows[kind], 16) if kind < kinds - 1 else 0
+            base = pl.multiple_of(me * rows[kind], 16)
             w_at = new_w[kind].at[layer]
 
             def adamw(r, _):
@@ -227,34 +234,109 @@
                 w_at[there] = (old - 0.02 * step).astype(jnp.bfloat16)
 
             each_rows(kind, adamw)
+            @pl.when(late)
+            def _():
+                for way in range(2):
+                    more.copy(way, 1, pieces[layer][kind]).start()
+
             if kind < kinds - 1:
-                for way in range(2):
-                    gather.send(way, 1, layer, kind)
-    gather.run()
+
+                @pl.when(jnp.logical_not(late))
+                def _():
+                    for way in range(2):
+                        some.copy(way, 1, pieces[layer][kind]).start()
+
+    @pl.when(late)
+    def _():
+        more.run(short=(kinds - 1,))
+
+    @pl.when(jnp.logical_not(late))
+    def _():
+        some.run()
+
     for kind in range(kinds):
         pltpu.make_async_copy(got[kind], got[kind], rs_send.at[kind]).wait()
     pltpu.make_async_copy(others, others, sq_send.at[0]).wait()
 
 
-def gather_last(n, own, after, out, arrived, sent):
-    me, at = meet(n)
-    gather = Gather(n, at, [out], [own.shape[1]], arrived, sent)
-    for i in range(own.shape[0]):
+def gather_last(n, begun, after, rest, arrived, sent):
+    me, at = ring(n)
+    late = ends_last()
+
+    @pl.when(jnp.logical_not(late))
+    def _():
+        pl.delay(PAUSE_NS)
+
+    meet(at)
+    layers, rows = begun.shape[0], begun.shape[1] // n
+    pieces = [(0, layer, 0, rows, layer * 2 // layers) for layer in range(layers)]
+    gather = Gather(n, at, [rest], [rows], [pieces[::step] for step in WAYS], arrived, sent)
+
+    def source(way, steps, layer):
+        return begun.at[layer, pl.ds(pl.multiple_of(at(way, -steps) * rows, 16), rows)]
+
+    @pl.when(late)
+    def _():
         for way in range(2):
-            layer = (*halved(own.shape[0], way), *halved(own.shape[0], 1 - way))[i]
-            gather.send(way, 1, layer, 0, own.at[layer])
-    out[:, gather.block(me, 0)] = own[...]
-    gather.run()
-
-
-def write_out(*refs):
-    n = (len(refs) - 2) // 2
-    copies = [pltpu.make_async_copy(src, dst, refs[-1].at[i]) for i, (src, dst) in enumerate(zip(refs[:n], refs[n : 2 * n]))]
-    refs[-2][...] = jnp.zeros_like(refs[-2])
+            for piece in gather.order(way, n // 2):
+                gather.copy(way, n // 2, piece, source(way, n // 2 - 1, piece[1])).start()
+        for way in range(2):
+            for piece in gather.order(way, n // 2):
+                gather.copy(way, n // 2, piece).wait_recv()
+        gather.wait_sent(0, 1)
+
+    @pl.when(jnp.logical_not(late))
+    def _():
+        for i in range(layers):
+            for way in range(2):
+                gather.copy(way, 1, gather.orders[way][i], source(way, 0, gather.orders[way][i][1])).start()
+        gather.run()
+
+
+def copy_blocks(n, src, dst, sem, offsets):
+    me, at = ring(n)
+    rows = src.shape[1] // n
+    blocks = [pl.ds(pl.multiple_of(at(0, off) * rows, 16), rows) for off in offsets]
+    return [pltpu.make_async_copy(src.at[:, here], dst.at[:, here], sem.at[off]) for here, off in zip(blocks, offsets)]
+
+
+def run_all(copies):
     for copy in copies:
         copy.start()
     for copy in copies:
         copy.wait()
+
+
+def write_most(n, *refs):
+    *refs, done, sems, block_sems = refs
+    whole = [pltpu.make_async_copy(src, dst, sems.at[i]) for i, (src, dst) in enumerate(zip(refs[:9], refs[9:])) if i != 2]
+    for copy in whole:
+        copy.start()
+    done[...] = jnp.zeros_like(done)
+    late = ends_last()
+
+    @pl.when(late)
+    def _():
+        run_all(copy_blocks(n, refs[2], refs[11], block_sems, [off for off in range(n) if off != n // 2]))
+
+    @pl.when(jnp.logical_not(late))
+    def _():
+        run_all(copy_blocks(n, refs[2], refs[11], block_sems, [0]))
+
+    for copy in whole:
+        copy.wait()
+
+
+def write_rest(n, rest, begun, out, sems):
+    late = ends_last()
+
+    @pl.when(late)
+    def _():
+        run_all(copy_blocks(n, rest, out, sems, [n // 2]))
+
+    @pl.when(jnp.logical_not(late))
+    def _():
+        run_all(copy_blocks(n, rest, out, sems, range(1, n)))
 
 
 def solution(mesh):
@@ -274,10 +356,10 @@
         scratch += [pltpu.VMEM((2, terms_kept, *s), jnp.bfloat16) for s in shapes]
         scratch += [pltpu.VMEM((2, sums, *s), jnp.bfloat16) for s in shapes]
         scratch += [pltpu.VMEM((n, 1, 128), jnp.float32)]
-        scratch += [dma((2, sums, 3)), dma((3,)), dma((2,)), dma((1,)), dma((1,)), dma((3,)), dma((3,)), dma((3, 3))]
+        scratch += [dma((2, 3 * sums)), dma((3,)), dma((3,)), dma((1,)), dma((1,)), dma((3,)), dma((3,)), dma((3, 3))]
         in_vmem, in_hbm = pl.BlockSpec(memory_space=pltpu.VMEM), pl.BlockSpec(memory_space=pltpu.HBM)
-        new = [*weights[:2], jax.ShapeDtypeStruct(m[2].shape, weights[2].dtype), *m, *v]
-        new = pl.pallas_call(
+        new = [*weights, *m, *v]
+        kept = pl.pallas_call(
             functools.partial(sum_and_step, n, layers, count),
             out_shape=[pltpu.VMEM(one.shape, one.dtype) for one in new],
             in_specs=[in_hbm] * 12,
@@ -285,27 +367,32 @@
             scratch_shapes=scratch,
             compiler_params=pltpu.CompilerParams(collective_id=0, has_side_effects=True, vmem_limit_bytes=40 * 2**20),
         )(*terms, *weights, *m, *v)
-
-        def written(*kept):
-            return pl.pallas_call(
-                write_out,
-                out_shape=[*(jax.ShapeDtypeStruct(one.shape, one.dtype) for one in kept), pltpu.VMEM((8, 128), jnp.float32)],
-                in_specs=[in_vmem] * len(kept),
-                out_specs=[in_hbm] * len(kept) + [in_vmem],
-                scratch_shapes=[dma((len(kept),))],
-                compiler_params=pltpu.CompilerParams(vmem_limit_bytes=2**20),
-            )(*kept)
-
-        gate, up, *moments, done = written(*new[:2], *new[3:])
-        down = pl.pallas_call(
+        *written, done = pl.pallas_call(
+            functools.partial(write_most, n),
+            out_shape=[*(jax.ShapeDtypeStruct(one.shape, one.dtype) for one in new), pltpu.VMEM((8, 128), jnp.float32)],
+            in_specs=[in_vmem] * 9,
+            out_specs=[in_hbm] * 9 + [in_vmem],
+            scratch_shapes=[dma((9,)), dma((n,))],
+            compiler_params=pltpu.CompilerParams(vmem_limit_bytes=2**20),
+        )(*kept)
+        rest = pl.pallas_call(
             functools.partial(gather_last, n),
             out_shape=pltpu.VMEM(weights[2].shape, weights[2].dtype),
             in_specs=[in_vmem, in_vmem],
             out_specs=in_vmem,
-            scratch_shapes=[dma((2, sums, 1)), dma((1,))],
+            scratch_shapes=[dma((2, half * layers)), dma((1,))],
             compiler_params=pltpu.CompilerParams(collective_id=1, has_side_effects=True, vmem_limit_bytes=2**20),
-        )(new[2], done)
-        return (gate, up, down, *moments)
+        )(kept[2], done)
+        written[2] = pl.pallas_call(
+            functools.partial(write_rest, n),
+            out_shape=jax.ShapeDtypeStruct(weights[2].shape, weights[2].dtype),
+            in_specs=[in_vmem, in_hbm],
+            out_specs=in_hbm,
+            input_output_aliases={1: 0},
+            scratch_shapes=[dma((n,))],
+            compiler_params=pltpu.CompilerParams(vmem_limit_bytes=2**20),
+        )(rest, written[2])
+        return tuple(written)
 
     all_of, cut = P(None, None, None), P(None, "dp", None)
     return jax.shard_map(

time: 233 us -> 232 us (level)
    pallas_call x1, Pallas kernels: 27.3 us -> 8.34 us  [step(): pl.pallas_call(functools.partial(gather_last, n), out_shape=pltpu.VMEM(we...]
    pallas_call x1, Pallas kernels: 198 us -> 216 us  [step(): pl.pallas_call(functools.partial(sum_and_step, n, layers, count), out_sha...]
    pallas_call x1 -> x2, Pallas kernels: 5.09 us -> 7.06 us  [the longest x1 6.2 us: step(): pl.pallas_call(functools.partial(write_most, n), out_shape=[*(jax.ShapeDt...]
where the time goes in v5:
time: 232 us
  Pallas kernels  231 us (100%)
    pallas_call x1, Pallas kernels, step(): pl.pallas_call(functools.partial(sum_and_step, n, layers, count), out_sha...  216 us
    pallas_call x1, Pallas kernels, step(): pl.pallas_call(functools.partial(gather_last, n), out_shape=pltpu.VMEM(we...  8.34 us
    pallas_call x1, Pallas kernels, step(): pl.pallas_call(functools.partial(write_most, n), out_shape=[*(jax.ShapeDt...  6.2 us

profile of v5, /device:TPU:22, one launch (start us, length us, event | category | flops | bytes accessed | tf_op | source)
XLA Modules:
  0.0 231.7 jit_solution(2403035706969827267)
XLA Ops:
  0.6 215.7 %shard_map.187 = (bf16[2,640,1536]{2,1,0:T(8,128)(2,1)S(1)}, bf16[2,640,1536]{2,1,0:T(8,128)(2,1)S(1)}, bf16[2,1536,640]{2,1,0:T(8,128)(2,1)S(1)}, f32[2,80,1536...) custom-call(bf16[2,640,1536]{2,1,0:T(8,128)(2,1)} %bitcast.3, ...), custom_call_target="tpu_custom_call" | custom-call | tf_op jit(solution)/shard_map/pallas_call | solution.py:362
  216.3 6.2 %shard_map.188 = (bf16[2,640,1536]{2,1,0:T(8,128)(2,1)}, bf16[2,640,1536]{2,1,0:T(8,128)(2,1)}, bf16[2,1536,640]{2,1,0:T(8,128)(2,1)}, f32[2,80,1536]{2,1,0:T(8,...) custom-call(bf16[2,640,1536]{2,1,0:T(8,128)(2,1)S(1)} %get-tuple-ele, ...), custom_call_target="tpu_custom_call" | custom-call | tf_op jit(solution)/shard_map/pallas_call | solution.py:370
  222.5 8.3 %shard_map.189.rest = bf16[2,1536,640]{2,1,0:T(8,128)(2,1)S(1)} custom-call(bf16[2,1536,640]{2,1,0:T(8,128)(2,1)S(1)} %get-tuple-element.30.refs_2_.begun, f32[8,128]{1,0:T(8,128)S(1)} %get-tuple-element.39.after), custom_call_target="tpu_custom_call" | custom-call | tf_op jit(solution)/shard_map/pallas_call | solution.py:378
  230.9 0.9 shard_map.190

commit v6 on v5

--- a/solution.py
+++ b/solution.py
@@ -9,7 +9,7 @@
 
 WAYS = (1, -1)
 LAG_NS = 4000
-PAUSE_NS = 11700
+PAUSE_NS = 11500
 
 
 def row_blocks(rows, columns):

time: 232 us -> 232 us (level)
  no operation moved by 1% of the time
where the time goes in v6:
time: 232 us
  Pallas kernels  231 us (100%)
    pallas_call x1, Pallas kernels, step(): pl.pallas_call(functools.partial(sum_and_step, n, layers, count), out_sha...  216 us
    pallas_call x1, Pallas kernels, step(): pl.pallas_call(functools.partial(gather_last, n), out_shape=pltpu.VMEM(we...  8.14 us
    pallas_call x1, Pallas kernels, step(): pl.pallas_call(functools.partial(write_most, n), out_shape=[*(jax.ShapeDt...  6.2 us

profile of v6, /device:TPU:22, one launch (start us, length us, event | category | flops | bytes accessed | tf_op | source)
XLA Modules:
  0.0 231.7 jit_solution(1895995034186590755)
XLA Ops:
  0.6 215.9 %shard_map.187 = (bf16[2,640,1536]{2,1,0:T(8,128)(2,1)S(1)}, bf16[2,640,1536]{2,1,0:T(8,128)(2,1)S(1)}, bf16[2,1536,640]{2,1,0:T(8,128)(2,1)S(1)}, f32[2,80,1536...) custom-call(bf16[2,640,1536]{2,1,0:T(8,128)(2,1)} %bitcast.3, ...), custom_call_target="tpu_custom_call" | custom-call | tf_op jit(solution)/shard_map/pallas_call | solution.py:362
  216.5 6.2 %shard_map.188 = (bf16[2,640,1536]{2,1,0:T(8,128)(2,1)}, bf16[2,640,1536]{2,1,0:T(8,128)(2,1)}, bf16[2,1536,640]{2,1,0:T(8,128)(2,1)}, f32[2,80,1536]{2,1,0:T(8,...) custom-call(bf16[2,640,1536]{2,1,0:T(8,128)(2,1)S(1)} %get-tuple-ele, ...), custom_call_target="tpu_custom_call" | custom-call | tf_op jit(solution)/shard_map/pallas_call | solution.py:370
  222.7 8.1 %shard_map.189.rest = bf16[2,1536,640]{2,1,0:T(8,128)(2,1)S(1)} custom-call(bf16[2,1536,640]{2,1,0:T(8,128)(2,1)S(1)} %get-tuple-element.30.refs_2_.begun, f32[8,128]{1,0:T(8,128)S(1)} %get-tuple-element.39.after), custom_call_target="tpu_custom_call" | custom-call | tf_op jit(solution)/shard_map/pallas_call | solution.py:378
  230.9 0.9 shard_map.190
